TPU v7x, 256 devices: a whole 4x4x8 slice. The times are simulated.
256 devices in a mesh: pop: 64 (over x, z, core), mp: 4 (over y).
Axes of the slice: x: 4, y: 4, z: 8, core: 2. Of those that a mesh axis runs over, the one named last changes fastest.
Arguments:
- tokens: bfloat16 [256, 3584], replicated, may hold values from -60 to 60
- target: bfloat16 [256, 3584], P(None, 'mp'), may hold values from -6 to 6
- w_query: bfloat16 [3584, 3584], P('pop', 'mp'), may hold values from -0.09375 to 0.09375
- w_key: bfloat16 [3584, 512], P(None, 'mp'), may hold values from -0.09375 to 0.09375
- w_value: bfloat16 [3584, 512], P(None, 'mp'), may hold values from -0.09375 to 0.09375
- w_out: bfloat16 [3584, 3584], P('mp', 'pop'), may hold values from -0.09375 to 0.09375
- query_left_factors: bfloat16 [64, 3584, 4], P('pop'), may hold values from -0.09375 to 0.09375
- query_right_factors: bfloat16 [64, 4, 3584], P('pop', None, 'mp'), may hold values from -6 to 6
- o_left: bfloat16 [64, 3584, 4], P('pop', 'mp'), may hold values from -0.09375 to 0.09375
- o_right: bfloat16 [64, 4, 3584], P('pop'), may hold values from -6 to 6
- member_ids: int32 [64], P('pop'), may hold values from 0 to 63, each once
Outputs:
- grad_query: float32 [3584, 3584], P('pop', 'mp')
- grad_out: float32 [3584, 3584], P('mp', 'pop')
- fitness: float32 [64], P('pop')
Inputs may be any that keep to these rules, and one draw needn't show every extreme that they name: `member_ids`: every number from 0 to 63 appears once.
All inputs are finite; a program needn't handle non-finite values.
Results may differ from a plain program's by a relative error of at most 0.005.
Values may be sent and summed in bfloat16 or wider, within the bound.
No kernel may reach another device: no remote copies, remote signals or barrier semaphores. Data moves between devices by JAX's collectives and lax.ppermute only.
A program may use at most 64 MiB of HBM per device.

v0:
```python
import math
import jax
import jax.numpy as jnp
from jax import lax
from jax.sharding import Mesh
from jax.sharding import PartitionSpec as P

D = 3584
HEADS = 28
KV_HEADS = 4
HEAD_DIM = 128
RANK = 4
POP = ("pop_0", "pop_1", "pop_2")
noise_scale = 0.5
rope_base = 1000000.0
spread_floor = 0.001


def in_order(parts, dim):
    parts = jnp.moveaxis(parts, 0, dim)
    shape = parts.shape
    return parts.reshape(*shape[:dim], shape[dim] * shape[dim + 1], *shape[dim + 2 :])


def all_blocks(shard, axes, turns):
    parts = shard[None]
    for k in turns:
        parts = lax.all_gather(parts, axes[k], axis=0, tiled=True)
    held = [lax.axis_size(axes[k]) for k in reversed(turns)]
    parts = parts.reshape(*held, *shard.shape)
    turned = sorted(range(len(turns)), key=lambda place: turns[len(turns) - 1 - place])
    return parts.transpose(*turned, *range(len(turns), parts.ndim)).reshape(-1, *shard.shape)


def whole_of(shard, axes, turns, dim):
    return in_order(all_blocks(shard, axes, turns), dim)


def cut_along(shard, dim, devices):
    before, after = (shard.shape[:dim], shard.shape[dim + 1 :])
    return jnp.moveaxis(shard.reshape(*before, devices, -1, *after), dim, 0)


def summed_on_arrival(shard, axis, dim):
    devices = lax.axis_size(axis)
    parts = lax.all_to_all(cut_along(shard, dim, devices), axis, 0, 0, tiled=True)
    return jnp.sum(parts.astype(jnp.float32), axis=0)


def copy_for_each(shard, axis):
    copies = jnp.broadcast_to(shard, (lax.axis_size(axis), *shard.shape))
    return lax.all_to_all(copies, axis, split_axis=0, concat_axis=0, tiled=True)


def of_everyone(shard, axis):
    return copy_for_each(shard, axis).sum(axis=0)


def gathered_copies(shard, axis, dim):
    return in_order(copy_for_each(shard, axis), dim)


def side_by_side(arrays, axis, dim, along):
    columns = [a.reshape(*a.shape[:along], -1) for a in arrays]
    both = jnp.concatenate(columns, axis=along)
    result, at, done = (lax.all_gather(both, axis, axis=dim, tiled=True), 0, [])
    for a, column in zip(arrays, columns):
        share = result[..., at : at + column.shape[along]]
        done.append(share.reshape(*share.shape[:along], *a.shape[along:]))
        at += column.shape[along]
    return tuple(done)


def tables(count, head_size):
    position = jnp.arange(count, dtype=jnp.float32)
    index = jnp.arange(head_size // 2, dtype=jnp.float32)
    freq = jnp.exp(-math.log(rope_base) * 2.0 * index / head_size)
    angle = position[:, None] * freq[None, :]
    return (jnp.cos(angle)[:, None, :], jnp.sin(angle)[:, None, :])


def rotate(field, cosine_table, sine):
    half = field.shape[-1] // 2
    first = field[..., :half]
    second = field[..., half:]
    return jnp.concatenate(
        [first * cosine_table - second * sine, second * cosine_table + first * sine], axis=-1
    )


def per_device(
    tokens,
    target,
    w_query,
    w_key,
    w_value,
    w_out,
    query_left_factors,
    query_right_factors,
    o_left,
    o_right,
    member_ids,
):
    tok = tokens.shape[0]
    local_feats = w_query.shape[1]
    local_kv = w_key.shape[1] // HEAD_DIM
    group = HEADS // KV_HEADS
    local_heads = local_kv * group
    slots = query_left_factors.shape[0]
    scale = HEAD_DIM ** (-0.5)
    cosine_table, sine = tables(tok, HEAD_DIM)
    base = jnp.dot(tokens, whole_of(w_query, POP, (0, 1, 2), 0), preferred_element_type=jnp.float32)
    keys = rotate(
        jnp.dot(tokens, w_key, preferred_element_type=jnp.float32).reshape(tok, local_kv, HEAD_DIM),
        cosine_table,
        sine,
    ).astype(jnp.bfloat16)
    values = (
        jnp.dot(tokens, w_value, preferred_element_type=jnp.float32)
        .astype(jnp.bfloat16)
        .reshape(tok, local_kv, HEAD_DIM)
    )
    signs = (1 - 2 * (member_ids % 2)).astype(jnp.float32)
    factor = noise_scale * signs[:, None, None]
    lowrank_product = jnp.einsum(
        "td,mdr->mtr", tokens, query_left_factors, preferred_element_type=jnp.float32
    ).astype(jnp.bfloat16)
    query = base[None] + factor * jnp.einsum(
        "olj,ojv->olv", lowrank_product, query_right_factors, preferred_element_type=jnp.float32
    )
    query = rotate(
        query.reshape(slots, tok, local_heads, HEAD_DIM), cosine_table[None], sine[None]
    ).astype(jnp.bfloat16)
    query = query.reshape(slots, tok, local_kv, group, HEAD_DIM)
    scores = jnp.einsum("mtkgd,skd->mkgts", query, keys, preferred_element_type=jnp.float32) * scale
    causal = jnp.arange(tok)[:, None] >= jnp.arange(tok)[None, :]
    scores = jnp.where(causal, scores, -1e30)
    probs = jax.nn.softmax(scores, axis=-1).astype(jnp.bfloat16)
    mixed = (
        jnp.einsum("mkgts,skd->mtkgd", probs, values, preferred_element_type=jnp.float32)
        .astype(jnp.bfloat16)
        .reshape(slots, tok, local_feats)
    )
    low_out = jnp.einsum("mtf,mfr->mtr", mixed, o_left, preferred_element_type=jnp.float32)
    right_full = o_right.astype(jnp.float32)
    part = jnp.einsum(
        "mtf,fe->mte",
        mixed,
        lax.all_gather(w_out, POP, axis=1, tiled=True),
        preferred_element_type=jnp.float32,
    )
    term = part + factor * jnp.einsum(
        "mtr,mre->mte", low_out, right_full, precision=lax.Precision.HIGHEST
    )
    output = summed_on_arrival(term.astype(jnp.bfloat16), "mp", 2)
    diff = output - target.astype(jnp.float32)[None]
    errors = of_everyone(jnp.sum(diff * diff, axis=(1, 2)), "mp")
    fitness = -(errors / (tok * D))
    count = slots * lax.axis_size(POP)
    everyone = gathered_copies(fitness, POP, 0)
    mean = jnp.sum(everyone) / count
    spread = jnp.sum((everyone - mean) * (everyone - mean)) / count
    weight = signs * (fitness - mean) / jnp.sqrt(spread + spread_floor)
    every_weight = gathered_copies(weight, POP, 0)
    right_factors_gathered, left_all = side_by_side((query_right_factors, o_left), POP, 0, 1)
    rows_q = lax.all_to_all(query_left_factors, POP, split_axis=1, concat_axis=0, tiled=True)
    cols_o = lax.all_to_all(o_right, POP, split_axis=2, concat_axis=0, tiled=True)
    whole_population = rows_q.shape[0]
    left_q = jnp.transpose(
        rows_q.astype(jnp.float32) * every_weight[:, None, None], (1, 0, 2)
    ).reshape(rows_q.shape[1], whole_population * RANK)
    right_q = right_factors_gathered.astype(jnp.float32).reshape(
        whole_population * RANK, local_feats
    )
    grad_query = jnp.dot(left_q, right_q, precision=lax.Precision.HIGHEST) / noise_scale
    output_left_factor = jnp.transpose(
        left_all.astype(jnp.float32) * every_weight[:, None, None], (1, 0, 2)
    ).reshape(local_feats, whole_population * RANK)
    right_o = cols_o.astype(jnp.float32).reshape(whole_population * RANK, cols_o.shape[2])
    grad_out = jnp.dot(output_left_factor, right_o, precision=lax.Precision.HIGHEST) / noise_scale
    return (grad_query, grad_out, fitness)


def solution(mesh):
    torus = Mesh(mesh.devices.reshape(4, 8, 2, mesh.shape["mp"]), ("pop_0", "pop_1", "pop_2", "mp"))
    placed = (
        P(),
        P(None, "mp"),
        P(POP, "mp"),
        P(None, "mp"),
        P(None, "mp"),
        P("mp", POP),
        P(POP, None, None),
        P(POP, None, "mp"),
        P(POP, "mp", None),
        P(POP, None, None),
        P(POP),
    )
    return jax.shard_map(
        per_device,
        mesh=torus,
        in_specs=placed,
        out_specs=(P(POP, "mp"), P("mp", POP), P(POP)),
        check_vma=False,
    )
```

profile of v0, /device:TPU:1, one launch (start us, length us, event | category | flops | bytes accessed | tf_op | source)
XLA Modules:
  0.0 428.7 jit_solution(7784847421207332163)
XLA Ops:
  7.2 13.0 %all-gather = bf16[224,896]{1,0:T(8,128)(2,1)} all-gather(bf16[56,896]{1,0:T(8,128)(2,1)} %param.13), channel_id=2, replica_groups=mesh['pop_0'=4,'pop_1'=8,'pop_2'=2,'mp'=4] {'pop_0'}, dimensions={0}, use_global_device_ids=true | all-gather | bytes 501760 | tf_op jit(solution)/shard_map/all_gather | solution.py:28
  20.3 49.6 %all-gather.6.cloned.1.call-done = bf16[32,56,896]{2,1,0:T(8,128)(2,1)} async-done(((bf16[4,56,896]{2,1,0:T(8,128)(2,1)}), bf16[32,56,896]{2,1,0:T(8,128)(2,1)}) %all-gather.6.cloned.1.call-update) | async-done | bytes 3211280 | tf_op jit(solution)/shard_map/all_gather | solution.py:28
  73.6 19.9 %all-gather.8.cloned.1.call-done = bf16[64,56,896]{2,1,0:T(8,128)(2,1)} async-done(((bf16[32,56,896]{2,1,0:T(8,128)(2,1)}), bf16[64,56,896]{2,1,0:T(8,128)(2,1)}) %all-gather.8.cloned.1.call-update) | async-done | bytes 6422544 | tf_op jit(solution)/shard_map/all_gather | solution.py:28
  93.5 3.3 copy.114
  96.9 2.1 fusion.29
  110.0 2.6 convolution_convert_fusion
  112.8 65.1 %all-gather.10.cloned.1.call-done = bf16[896,3584]{0,1:T(8,128)(2,1)} async-done(((bf16[896,56]{0,1:T(8,128)(2,1)}), bf16[896,3584]{0,1:T(8,128)(2,1)}) %all-gather.10.cloned.1.call-update) | async-done | bytes 6422544 | tf_op jit(solution)/shard_map/all_gather | solution.py:149
  177.9 4.9 %fusion.30 = f32[256,3584]{1,0:T(8,128)S(1)} fusion(bf16[256,896]{0,1:T(8,128)(2,1)S(1)} %bitcast.106, bf16[896,3584]{0,1:T(8,128)(2,1)} %all-gather.10.cloned.1.call-done), kind=kOutput, calls=%fused_computation.58 | convolution fusion | flops 1644167168 | bytes 10551296 | tf_op jit(solution)/shard_map/mtf,fe->mte/dot_general | solution.py:146
  182.8 3.1 fusion.1
  185.9 3.3 reshape.288
  190.7 4.0 all-to-all-start.1
  195.3 22.5 %all-to-all-done.1 = bf16[4,1,256,896]{3,2,1,0:T(8,128)(2,1)S(1)} async-done(((bf16[4,1,256,896]{3,2,1,0:T(8,128)(2,1)}), bf16[4,1,256,896]{3,2,1,0:T(8,128)(2,1)S(1)}, u32[]{:S(2)}, u32[]{:S(2)}) %all-to-all-start.1) | async-done | bytes 1835040 | tf_op jit(solution)/shard_map/all_to_all | solution.py:46
  219.6 6.5 %all_to_all.47 = f32[4,1,1]{2,1,0:T(1,128)S(1)} all-to-all(f32[4,1,1]{2,1,0:T(1,128)S(1)} %broadcast_in_dim.34), channel_id=1, replica_groups=mesh['pop_0'=4,'pop_1'=8,'pop_2'=2,'mp'=4] {'mp'}, dimensions={0} | all-to-all | bytes 32 | tf_op jit(solution)/shard_map/all_to_all | solution.py:52
  227.9 7.9 %all-to-all-start.3 = ((f32[64,1,1]{2,1,0:T(1,128)}), f32[64,1,1]{2,1,0:T(1,128)S(1)}, u32[]{:S(2)}, u32[]{:S(2)}) async-start(f32[64,1,1]{2,1,0:T(1,128)} %broadcast_in_dim.35), calls=%async_computation.3 | async-start | bytes 65536 | tf_op jit(solution)/shard_map/all_to_all | solution.py:52
  235.9 51.8 %all-gather.1 = bf16[64,1,7168]{2,1,0:T(2,128)(2,1)S(1)} all-gather(bf16[1,1,7168]{2,1,0:T(2,128)(2,1)S(1)} %maximum_bitcast_fusion.2), channel_id=1, replica_groups=mesh['pop_0'=4,'pop_1'=8,'pop_2'=2,'mp'=4] {'pop_0','pop_1','pop_2'}, dimensions={0}, use_global_device_ids=true | all-gather | bytes 931840 | tf_op jit(solution)/shard_map/all_gather | solution.py:66
  287.7 3.2 copy.129
  292.2 7.3 %all-to-all-start.5 = ((bf16[1,4,3584]{1,0,2:T(2,128)(2,1)}), bf16[1,4,3584]{1,0,2:T(2,128)(2,1)S(1)}, u32[]{:S(2)}, u32[]{:S(2)}) async-start(bf16[1,4,3584]{1,0,2:T(2,128)(2,1)} %copy.129), calls=%async_computation.5 | async-start | bytes 3670016 | tf_op jit(solution)/shard_map/all_to_all | solution.py:167
  301.5 3.2 copy.112
  306.1 38.7 %all-to-all-done.5 = bf16[1,4,3584]{1,0,2:T(2,128)(2,1)S(1)} async-done(((bf16[1,4,3584]{1,0,2:T(2,128)(2,1)}), bf16[1,4,3584]{1,0,2:T(2,128)(2,1)S(1)}, u32[]{:S(2)}, u32[]{:S(2)}) %all-to-all-start.5) | async-done | bytes 28704 | tf_op jit(solution)/shard_map/all_to_all | solution.py:167
  344.8 6.2 %all-to-all-start = ((bf16[1,3584,4]{2,0,1:T(2,128)(2,1)}), bf16[1,3584,4]{2,0,1:T(2,128)(2,1)}, u32[]{:S(2)}, u32[]{:S(2)}) async-start(bf16[1,3584,4]{2,0,1:T(2,128)(2,1)} %copy.112), calls=%async_computation | async-start | bytes 3670016 | tf_op jit(solution)/shard_map/all_to_all | solution.py:166
  352.3 44.0 %all-to-all-done = bf16[1,3584,4]{2,0,1:T(2,128)(2,1)} async-done(((bf16[1,3584,4]{2,0,1:T(2,128)(2,1)}), bf16[1,3584,4]{2,0,1:T(2,128)(2,1)}, u32[]{:S(2)}, u32[]{:S(2)}) %all-to-all-start) | async-done | bytes 28704 | tf_op jit(solution)/shard_map/all_to_all | solution.py:166
  396.9 6.0 %all-to-all-start.4 = ((f32[64,1,1]{2,1,0:T(1,128)}), f32[64,1,1]{2,1,0:T(1,128)S(1)}, u32[]{:S(2)}, u32[]{:S(2)}) async-start(f32[64,1,1]{2,1,0:T(1,128)} %broadcast_in_dim.36), calls=%async_computation.4 | async-start | bytes 65536 | tf_op jit(solution)/shard_map/all_to_all | solution.py:52
  408.1 3.7 copy.113
  414.4 2.8 copy.128
  (79 shorter events, 35.9 us)
Async XLA Ops:
  7.2 64.2 %copy-start = (bf16[256,3584]{1,0:T(8,128)(2,1)S(1)}, bf16[256,3584]{1,0:T(8,128)(2,1)}, u32[]{:S(2)}) copy-start(bf16[256,3584]{1,0:T(8,128)(2,1)} %param.11) | copy-start | bytes 5505028
  7.2 62.7 %all-gather.6.cloned.1.call-start = ((), (), s32[]{:S(2)}) async-start(), calls=%async_computation.6 | async-start | bytes 3612672 | tf_op jit(solution)/shard_map/all_gather | solution.py:28
  20.2 51.2 %copy-start.4 = (bf16[3584,128]{1,0:T(8,128)(2,1)S(1)}, bf16[3584,128]{1,0:T(8,128)(2,1)}, u32[]{:S(2)}) copy-start(bf16[3584,128]{1,0:T(8,128)(2,1)} %param.14) | copy-start | bytes 2752516
  20.3 73.3 %all-gather.8.cloned.1.call-start = ((), (), s32[]{:S(2)}) async-start(), calls=%async_computation.7 | async-start | bytes 9633792 | tf_op jit(solution)/shard_map/all_gather | solution.py:28
  69.9 107.9 %all-gather.10.cloned.1.call-start = ((), (), s32[]{:S(2)}) async-start(), calls=%async_computation.8 | async-start | bytes 6522880 | tf_op jit(solution)/shard_map/all_gather | solution.py:149
  96.9 2.2 copy-start.9
  96.9 2.2 copy-start.11
  106.1 1.4 copy-start.6
  106.1 1.4 copy-start.7
  108.1 1.3 copy-start.2
  108.2 1.9 copy-start.13
  110.0 2.6 copy-start.12
  112.8 70.0 %copy-start.8 = (bf16[1,4,3584]{2,1,0:T(4,128)(2,1)S(1)}, bf16[1,4,3584]{2,1,0:T(4,128)(2,1)}, u32[]{:S(2)}) copy-start(bf16[1,4,3584]{2,1,0:T(4,128)(2,1)} %param.20) | copy-start | bytes 86020
  190.7 27.1 %all-to-all-start.1 = ((bf16[4,1,256,896]{3,2,1,0:T(8,128)(2,1)}), bf16[4,1,256,896]{3,2,1,0:T(8,128)(2,1)S(1)}, u32[]{:S(2)}, u32[]{:S(2)}) async-start(bf16[4,1,256,896]{3,2,1,0:T(8,128)(2,1)} %bitcast.98), calls=%async_computation.1 | async-start | bytes 3670016 | tf_op jit(solution)/shard_map/all_to_all | solution.py:46
  194.7 23.3 %copy-start.5 = (bf16[256,896]{1,0:T(8,128)(2,1)S(1)}, bf16[256,896]{1,0:T(8,128)(2,1)}, u32[]{:S(2)}) copy-start(bf16[256,896]{1,0:T(8,128)(2,1)} %param.12) | copy-start | bytes 1376260
  227.9 64.2 %all-to-all-start.3 = ((f32[64,1,1]{2,1,0:T(1,128)}), f32[64,1,1]{2,1,0:T(1,128)S(1)}, u32[]{:S(2)}, u32[]{:S(2)}) async-start(f32[64,1,1]{2,1,0:T(1,128)} %broadcast_in_dim.35), calls=%async_computation.3 | async-start | bytes 65536 | tf_op jit(solution)/shard_map/all_to_all | solution.py:52
  292.2 52.6 %all-to-all-start.5 = ((bf16[1,4,3584]{1,0,2:T(2,128)(2,1)}), bf16[1,4,3584]{1,0,2:T(2,128)(2,1)S(1)}, u32[]{:S(2)}, u32[]{:S(2)}) async-start(bf16[1,4,3584]{1,0,2:T(2,128)(2,1)} %copy.129), calls=%async_computation.5 | async-start | bytes 3670016 | tf_op jit(solution)/shard_map/all_to_all | solution.py:167
  299.4 2.1 copy-start.10
  344.8 51.5 %all-to-all-start = ((bf16[1,3584,4]{2,0,1:T(2,128)(2,1)}), bf16[1,3584,4]{2,0,1:T(2,128)(2,1)}, u32[]{:S(2)}, u32[]{:S(2)}) async-start(bf16[1,3584,4]{2,0,1:T(2,128)(2,1)} %copy.112), calls=%async_computation | async-start | bytes 3670016 | tf_op jit(solution)/shard_map/all_to_all | solution.py:166
  396.9 15.3 %all-to-all-start.4 = ((f32[64,1,1]{2,1,0:T(1,128)}), f32[64,1,1]{2,1,0:T(1,128)S(1)}, u32[]{:S(2)}, u32[]{:S(2)}) async-start(f32[64,1,1]{2,1,0:T(1,128)} %broadcast_in_dim.36), calls=%async_computation.4 | async-start | bytes 65536 | tf_op jit(solution)/shard_map/all_to_all | solution.py:52
  407.9 4.9 %copy-start.3 = (f32[64,3584]{0,1:T(8,128)S(1)}, f32[64,3584]{0,1:T(8,128)}, u32[]{:S(2)}) copy-start(f32[64,3584]{0,1:T(8,128)} %copy.127) | copy-start | bytes 2752516
  414.3 6.7 %copy-start.1 = (bf16[256,3584]{1,0:T(8,128)(2,1)S(1)}, bf16[256,3584]{1,0:T(8,128)(2,1)}, u32[]{:S(2)}) copy-start(bf16[256,3584]{1,0:T(8,128)(2,1)} %param.11) | copy-start | bytes 5505028
Sparse Core Ops, SparseCore 0:
  20.4 49.4 all-gather.5
  71.7 21.7 all-gather.7
  96.2 81.5 all-gather.9
where the time goes:
time: 430 us; the launch traced here: 429 us
  waiting for transfers between devices  241 us (56%)
  blocking collectives  71.3 us (17%)
  local copies, waits for them, and re-layouts  38.2 us (9%)
  starting transfers between devices  31.5 us (7%)
  matrix products  18.6 us (4%)
  between operations  17.9 us (4%)
  other arithmetic  10.5 us (2%)
    all_gather x2, waiting for transfers between devices, all_blocks(): parts = lax.all_gather(parts, axes[k], axis=0, tiled=True)  69.5 us
    all_gather x1, waiting for transfers between devices, per_device(): lax.all_gather(w_out, POP, axis=1, tiled=True)  65.1 us
    all_gather x1, blocking collectives, side_by_side(): result, at, done = (lax.all_gather(both, axis, axis=dim, tiled=True), 0, [])  51.8 us
    all_to_all x1, waiting for transfers between devices, per_device(): lax.all_to_all(query_left_factors, POP, split_axis=1, concat_axis=0, tile...  44 us
    all_to_all x1, waiting for transfers between devices, per_device(): lax.all_to_all(o_right, POP, split_axis=2, concat_axis=0, tiled=True)  38.7 us
    all_to_all x1, waiting for transfers between devices, summed_on_arrival(): lax.all_to_all(cut_along(shard, dim, devices), axis, 0, 0, tiled=True)  22.5 us
    all_to_all x2, starting transfers between devices, copy_for_each(): return lax.all_to_all(copies, axis, split_axis=0, concat_axis=0, tiled=True)  14 us
    all_gather x1, blocking collectives, all_blocks(): parts = lax.all_gather(parts, axes[k], axis=0, tiled=True)  13 us
  transfers between devices with their start and end apart: 8, of which 7 were waited for; matrix products, arithmetic and copies ran while one was open for 9% of the time, Pallas kernels for 0%

commit v1 on v0

--- a/solution.py
+++ b/solution.py
@@ -164,7 +164,9 @@
     every_weight = gathered_copies(weight, POP, 0)
     right_factors_gathered, left_all = side_by_side((query_right_factors, o_left), POP, 0, 1)
     rows_q = lax.all_to_all(query_left_factors, POP, split_axis=1, concat_axis=0, tiled=True)
-    cols_o = lax.all_to_all(o_right, POP, split_axis=2, concat_axis=0, tiled=True)
+    pieces = jnp.split(o_right, lax.axis_size(POP), axis=2)
+    got = lax.all_to_all(jnp.stack(pieces), POP, 0, 0)
+    cols_o = jnp.concatenate(got, axis=0)
     whole_population = rows_q.shape[0]
     left_q = jnp.transpose(
         rows_q.astype(jnp.float32) * every_weight[:, None, None], (1, 0, 2)

time: 430 us -> 355 us (0.83)
  waiting for transfers between devices: 241 us -> 123 us
  local copies, waits for them, and re-layouts: 38.2 us -> 75.5 us
    all_gather x1, waiting for transfers between devices: 65.1 us -> 0.01 us  [per_device(): lax.all_gather(w_out, POP, axis=1, tiled=True)]
    all_to_all x1, waiting for transfers between devices: 38.7 us -> 1.74 us  [per_device(): got = lax.all_to_all(jnp.stack(pieces), POP, 0, 0)]
    unnamed x35 -> x97, local copies, waits for them, and re-layouts: 12 us -> 48.5 us
    all_gather x2, waiting for transfers between devices: 69.5 us -> 49.6 us  [all_blocks(): parts = lax.all_gather(parts, axes[k], axis=0, tiled=True)]
    all_to_all x2, waiting for transfers between devices: 0.2 us -> 7.13 us  [copy_for_each(): return lax.all_to_all(copies, axis, split_axis=0, concat_axis=0, tiled=True)]
  transfers between devices with their start and end apart: 8 -> 8, of which waited for: 7 -> 6; matrix products, arithmetic and copies ran while one was open for 9% -> 24% of each run, Pallas kernels for 0% -> 0%
where the time goes in v1:
time: 355 us; the launch traced here: 353 us
  waiting for transfers between devices  123 us (35%)
  local copies, waits for them, and re-layouts  75.5 us (21%)
  blocking collectives  70.9 us (20%)
  starting transfers between devices  34 us (10%)
  matrix products  18.8 us (5%)
  between operations  17.8 us (5%)
  other arithmetic  13.4 us (4%)
    all_gather x1, blocking collectives, side_by_side(): result, at, done = (lax.all_gather(both, axis, axis=dim, tiled=True), 0, [])  51.4 us
    all_gather x2, waiting for transfers between devices, all_blocks(): parts = lax.all_gather(parts, axes[k], axis=0, tiled=True)  49.6 us
    unnamed x97, local copies, waits for them, and re-layouts  48.5 us
    all_to_all x1, waiting for transfers between devices, per_device(): lax.all_to_all(query_left_factors, POP, split_axis=1, concat_axis=0, tile...  42.7 us
    all_to_all x1, waiting for transfers between devices, summed_on_arrival(): lax.all_to_all(cut_along(shard, dim, devices), axis, 0, 0, tiled=True)  21.1 us
    all_to_all x2, starting transfers between devices, copy_for_each(): return lax.all_to_all(copies, axis, split_axis=0, concat_axis=0, tiled=True)  15.2 us
    all_gather x1, blocking collectives, all_blocks(): parts = lax.all_gather(parts, axes[k], axis=0, tiled=True)  13 us
    all_to_all x1, starting transfers between devices, per_device(): got = lax.all_to_all(jnp.stack(pieces), POP, 0, 0)  8.61 us
  transfers between devices with their start and end apart: 8, of which 6 were waited for; matrix products, arithmetic and copies ran while one was open for 24% of the time, Pallas kernels for 0%

profile of v1, /device:TPU:1, one launch (start us, length us, event | category | flops | bytes accessed | tf_op | source)
XLA Modules:
  0.0 353.4 jit_solution(6779498463947155787)
XLA Ops:
  7.2 13.0 %all-gather = bf16[224,896]{1,0:T(8,128)(2,1)} all-gather(bf16[56,896]{1,0:T(8,128)(2,1)} %param.13), channel_id=2, replica_groups=mesh['pop_0'=4,'pop_1'=8,'pop_2'=2,'mp'=4] {'pop_0'}, dimensions={0}, use_global_device_ids=true | all-gather | bytes 501760 | tf_op jit(solution)/shard_map/all_gather | solution.py:28
  20.3 49.6 %all-gather.6.cloned.1.call-done = bf16[32,56,896]{2,1,0:T(8,128)(2,1)} async-done(((bf16[4,56,896]{2,1,0:T(8,128)(2,1)}), bf16[32,56,896]{2,1,0:T(8,128)(2,1)}) %all-gather.6.cloned.1.call-update) | async-done | bytes 3211280 | tf_op jit(solution)/shard_map/all_gather | solution.py:28
  72.6 51.4 %all-gather.1 = bf16[64,1,7168]{2,1,0:T(2,128)(2,1)S(1)} all-gather(bf16[1,1,7168]{2,1,0:T(2,128)(2,1)S(1)} %maximum_bitcast_fusion.2), channel_id=1, replica_groups=mesh['pop_0'=4,'pop_1'=8,'pop_2'=2,'mp'=4] {'pop_0','pop_1','pop_2'}, dimensions={0}, use_global_device_ids=true | all-gather | bytes 931840 | tf_op jit(solution)/shard_map/all_gather | solution.py:66
  165.2 3.4 copy.100
  168.7 2.1 fusion.29
  170.8 2.1 fusion.3
  181.8 2.6 convolution_convert_fusion
  184.5 5.2 %fusion.30 = f32[256,3584]{1,0:T(8,128)S(1)} fusion(bf16[256,896]{0,1:T(8,128)(2,1)S(1)} %bitcast.234, bf16[896,3584]{0,1:T(8,128)(2,1)} %all-gather.10.cloned.1.call-done), kind=kOutput, calls=%fused_computation.122 | convolution fusion | flops 1644167168 | bytes 10551296 | tf_op jit(solution)/shard_map/mtf,fe->mte/dot_general | solution.py:146
  189.7 3.1 fusion.1
  192.8 4.2 %reshape.289 = bf16[1,256,4,896]{3,2,1,0:T(4,128)(2,1)} reshape(bf16[256,3584]{1,0:T(8,128)(2,1)} %fusion.1) | data formatting | bytes 3670016 | tf_op jit(solution)/shard_map/reshape | solution.py:41
  197.1 3.0 copy.128
  200.0 4.5 %all-to-all-start.1 = ((bf16[4,1,256,896]{3,2,1,0:T(8,128)(2,1)}), bf16[4,1,256,896]{3,2,1,0:T(8,128)(2,1)}, u32[]{:S(2)}, u32[]{:S(2)}) async-start(bf16[4,1,256,896]{3,2,1,0:T(8,128)(2,1)} %bitcast.227), calls=%async_computation.1 | async-start | bytes 3670016 | tf_op jit(solution)/shard_map/all_to_all | solution.py:46
  207.0 21.1 %all-to-all-done.1 = bf16[4,1,256,896]{3,2,1,0:T(8,128)(2,1)} async-done(((bf16[4,1,256,896]{3,2,1,0:T(8,128)(2,1)}), bf16[4,1,256,896]{3,2,1,0:T(8,128)(2,1)}, u32[]{:S(2)}, u32[]{:S(2)}) %all-to-all-start.1) | async-done | bytes 1835040 | tf_op jit(solution)/shard_map/all_to_all | solution.py:46
  231.5 6.5 %all_to_all.37 = f32[4,1,1]{2,1,0:T(1,128)S(1)} all-to-all(f32[4,1,1]{2,1,0:T(1,128)S(1)} %broadcast_in_dim.34), channel_id=1, replica_groups=mesh['pop_0'=4,'pop_1'=8,'pop_2'=2,'mp'=4] {'mp'}, dimensions={0} | all-to-all | bytes 32 | tf_op jit(solution)/shard_map/all_to_all | solution.py:52
  239.9 9.1 %all-to-all-start.3 = ((f32[64,1,1]{2,1,0:T(1,128)}), f32[64,1,1]{2,1,0:T(1,128)S(1)}, u32[]{:S(2)}, u32[]{:S(2)}) async-start(f32[64,1,1]{2,1,0:T(1,128)} %broadcast_in_dim.35), calls=%async_computation.3 | async-start | bytes 65536 | tf_op jit(solution)/shard_map/all_to_all | solution.py:52
  249.7 3.2 copy.98
  252.9 5.4 %all-to-all-done.3 = f32[64,1,1]{2,1,0:T(1,128)S(1)} async-done(((f32[64,1,1]{2,1,0:T(1,128)}), f32[64,1,1]{2,1,0:T(1,128)S(1)}, u32[]{:S(2)}, u32[]{:S(2)}) %all-to-all-start.3) | async-done | bytes 288 | tf_op jit(solution)/shard_map/all_to_all | solution.py:52
  258.3 5.6 %all-to-all-start = ((bf16[1,3584,4]{2,0,1:T(2,128)(2,1)}), bf16[1,3584,4]{2,0,1:T(2,128)(2,1)}, u32[]{:S(2)}, u32[]{:S(2)}) async-start(bf16[1,3584,4]{2,0,1:T(2,128)(2,1)} %copy.98), calls=%async_computation | async-start | bytes 3670016 | tf_op jit(solution)/shard_map/all_to_all | solution.py:166
  266.6 42.7 %all-to-all-done = bf16[1,3584,4]{2,0,1:T(2,128)(2,1)} async-done(((bf16[1,3584,4]{2,0,1:T(2,128)(2,1)}), bf16[1,3584,4]{2,0,1:T(2,128)(2,1)}, u32[]{:S(2)}, u32[]{:S(2)}) %all-to-all-start) | async-done | bytes 28704 | tf_op jit(solution)/shard_map/all_to_all | solution.py:166
  309.9 6.0 %all-to-all-start.4 = ((f32[64,1,1]{2,1,0:T(1,128)}), f32[64,1,1]{2,1,0:T(1,128)S(1)}, u32[]{:S(2)}, u32[]{:S(2)}) async-start(f32[64,1,1]{2,1,0:T(1,128)} %broadcast_in_dim.36), calls=%async_computation.4 | async-start | bytes 65536 | tf_op jit(solution)/shard_map/all_to_all | solution.py:52
  319.6 3.6 %copy.99 = bf16[1,3584,4]{1,2,0:T(4,128)(2,1)S(1)} copy(bf16[1,3584,4]{2,0,1:T(2,128)(2,1)} %all-to-all-done) | data formatting | bytes 57344 | tf_op jit(solution)/shard_map/all_to_all | solution.py:166
  325.1 8.6 %all-to-all-start.5 = ((bf16[64,1,4,56]{3,2,1,0:T(4,128)(2,1)}), bf16[64,1,4,56]{3,2,1,0:T(4,128)(2,1)S(1)}, u32[]{:S(2)}, u32[]{:S(2)}) async-start(bf16[64,1,4,56]{3,2,1,0:T(4,128)(2,1)} %constant_dynamic-update-slice_fusion), calls=%async_computation.5 | async-start | bytes 131072 | tf_op jit(solution)/shard_map/all_to_all | solution.py:168
  334.3 3.1 multiply_bitcast_fusion
  337.5 2.7 copy.114
  (139 shorter events, 73.7 us)
Async XLA Ops:
  7.2 155.8 %copy-start = (bf16[256,3584]{1,0:T(8,128)(2,1)S(1)}, bf16[256,3584]{1,0:T(8,128)(2,1)}, u32[]{:S(2)}) copy-start(bf16[256,3584]{1,0:T(8,128)(2,1)} %param.11) | copy-start | bytes 5505028
  7.2 62.7 %all-gather.6.cloned.1.call-start = ((), (), s32[]{:S(2)}) async-start(), calls=%async_computation.6 | async-start | bytes 3612672 | tf_op jit(solution)/shard_map/all_gather | solution.py:28
  20.2 51.8 %copy-start.12 = (bf16[1,896,4]{1,2,0:T(4,128)(2,1)S(1)}, bf16[1,896,4]{1,2,0:T(4,128)(2,1)}, u32[]{:S(2)}) copy-start(bf16[1,896,4]{1,2,0:T(4,128)(2,1)} %param.19) | copy-start | bytes 21508
  20.3 145.0 %all-gather.8.cloned.1.call-start = ((), (), s32[]{:S(2)}) async-start(), calls=%async_computation.7 | async-start | bytes 9633792 | tf_op jit(solution)/shard_map/all_gather | solution.py:28
  69.9 2.6 copy-start.11
  69.9 114.6 %all-gather.10.cloned.1.call-start = ((), (), s32[]{:S(2)}) async-start(), calls=%async_computation.8 | async-start | bytes 6522880 | tf_op jit(solution)/shard_map/all_gather | solution.py:149
  124.0 1.2 copy-start.6
  124.0 39.0 %copy-start.4 = (bf16[3584,128]{1,0:T(8,128)(2,1)S(1)}, bf16[3584,128]{1,0:T(8,128)(2,1)}, u32[]{:S(2)}) copy-start(bf16[3584,128]{1,0:T(8,128)(2,1)} %param.14) | copy-start | bytes 2752516
  168.7 2.1 copy-start.9
  177.9 1.5 copy-start.7
  177.9 1.5 copy-start.8
  180.0 1.3 copy-start.1
  180.0 1.8 copy-start.13
  200.0 5.8 %copy-start.2 = (bf16[64,1,7168]{2,0,1:T(8,128)(2,1)S(1)}, bf16[64,1,7168]{2,0,1:T(8,128)(2,1)}, u32[]{:S(2)}) copy-start(bf16[64,1,7168]{2,0,1:T(8,128)(2,1)} %copy.129) | copy-start | bytes 2752516
  200.0 28.1 %all-to-all-start.1 = ((bf16[4,1,256,896]{3,2,1,0:T(8,128)(2,1)}), bf16[4,1,256,896]{3,2,1,0:T(8,128)(2,1)}, u32[]{:S(2)}, u32[]{:S(2)}) async-start(bf16[4,1,256,896]{3,2,1,0:T(8,128)(2,1)} %bitcast.227), calls=%async_computation.1 | async-start | bytes 3670016 | tf_op jit(solution)/shard_map/all_to_all | solution.py:46
  207.0 23.0 %copy-start.5 = (bf16[256,896]{1,0:T(8,128)(2,1)S(1)}, bf16[256,896]{1,0:T(8,128)(2,1)}, u32[]{:S(2)}) copy-start(bf16[256,896]{1,0:T(8,128)(2,1)} %param.12) | copy-start | bytes 1376260
  207.0 42.6 %copy-start.10 = (bf16[1,3584,4]{1,2,0:T(4,128)(2,1)S(1)}, bf16[1,3584,4]{1,2,0:T(4,128)(2,1)}, u32[]{:S(2)}) copy-start(bf16[1,3584,4]{1,2,0:T(4,128)(2,1)} %param.17) | copy-start | bytes 86020
  239.9 18.4 %all-to-all-start.3 = ((f32[64,1,1]{2,1,0:T(1,128)}), f32[64,1,1]{2,1,0:T(1,128)S(1)}, u32[]{:S(2)}, u32[]{:S(2)}) async-start(f32[64,1,1]{2,1,0:T(1,128)} %broadcast_in_dim.35), calls=%async_computation.3 | async-start | bytes 65536 | tf_op jit(solution)/shard_map/all_to_all | solution.py:52
  252.9 63.7 %copy-start.3 = (f32[64,3584]{1,0:T(8,128)S(1)}, f32[64,3584]{1,0:T(8,128)}, u32[]{:S(2)}) copy-start(f32[64,3584]{1,0:T(8,128)} %get-tuple-element.5) | copy-start | bytes 2752516
  258.3 51.0 %all-to-all-start = ((bf16[1,3584,4]{2,0,1:T(2,128)(2,1)}), bf16[1,3584,4]{2,0,1:T(2,128)(2,1)}, u32[]{:S(2)}, u32[]{:S(2)}) async-start(bf16[1,3584,4]{2,0,1:T(2,128)(2,1)} %copy.98), calls=%async_computation | async-start | bytes 3670016 | tf_op jit(solution)/shard_map/all_to_all | solution.py:166
  309.9 15.3 %all-to-all-start.4 = ((f32[64,1,1]{2,1,0:T(1,128)}), f32[64,1,1]{2,1,0:T(1,128)S(1)}, u32[]{:S(2)}, u32[]{:S(2)}) async-start(f32[64,1,1]{2,1,0:T(1,128)} %broadcast_in_dim.36), calls=%async_computation.4 | async-start | bytes 65536 | tf_op jit(solution)/shard_map/all_to_all | solution.py:52
  325.1 18.4 %all-to-all-start.5 = ((bf16[64,1,4,56]{3,2,1,0:T(4,128)(2,1)}), bf16[64,1,4,56]{3,2,1,0:T(4,128)(2,1)S(1)}, u32[]{:S(2)}, u32[]{:S(2)}) async-start(bf16[64,1,4,56]{3,2,1,0:T(4,128)(2,1)} %constant_dynamic-update-slice_fusion), calls=%async_computation.5 | async-start | bytes 131072 | tf_op jit(solution)/shard_map/all_to_all | solution.py:168
Sparse Core Ops, SparseCore 0:
  20.4 49.4 all-gather.5
  71.7 21.7 all-gather.7
  96.2 81.9 all-gather.9
